TPU v7x, 32 devices: a whole 2x2x4 slice. The times are simulated.
32 devices in a mesh: wave: 8 (over z, y), lev: 4 (over x, core).
Axes of the slice: x: 2, y: 2, z: 4, core: 2. Of those that a mesh axis runs over, the one named last changes fastest.
Arguments:
- spectral: bfloat16 [32, 6, 64, 1280], P('wave', None, 'lev'), may hold values from -0.01171875 to 0.01171875
- legendre: bfloat16 [32, 640, 1280], P('wave'), may hold values from -4 to 4
- wave_ids: int32 [32], replicated, may hold values from 0 to 1279, as said below
- trunc_lengths: int32 [32], replicated, may hold values from 1 to 1280, as said below
- cycle_points: int32 [1280], replicated, may hold values from 20 to 2560, as said below
- grid_coef: float32 [1280, 2560], P('wave'), may hold values from -6 to 6
- cycle_weights: float32 [640], replicated, may hold values from 0.1 to 2
- modes_in: bfloat16 [64, 64], replicated, may hold values from -0.75 to 0.75
- modes_out: bfloat16 [64, 64], replicated, may hold values from -0.75 to 0.75
- depths: float32 [64], replicated, may hold values from 0.05 to 20
Outputs:
- update: bfloat16 [32, 6, 64, 1280], P('wave', None, 'lev')
Inputs may be any that keep to these rules, and one draw needn't show every extreme that they name: `wave_ids`: distinct zonal wavenumbers; one slot holds wavenumber 0. `trunc_lengths`: the length of slot m is at most 1280 minus wave_ids[m] and at least half of that; the slot of wavenumber 0 has length 1280. `cycle_points`: multiples of 4; cycle j and cycle 1280 - 1-j have the same count; cycles near the equator have 2560.
All inputs are finite; a program needn't handle non-finite values.
Results may differ from a plain program's by a relative error of at most 0.011.
Values may be sent and summed in bfloat16 or wider, within the bound.
No kernel may reach another device: no remote copies, remote signals or barrier semaphores. Data moves between devices by JAX's collectives and lax.ppermute only.
A program may use at most 128 MiB of HBM per device.

v0:
```python
import jax
import jax.numpy as jnp
from jax import lax
from jax.sharding import PartitionSpec as P

NT = 1280


def trig_rows(wave_ids, cycle_count, lon_max):
    low_len = 64
    high_len = lon_max // low_len
    counts = cycle_count[:, None, None]
    count_float = counts.astype(jnp.float32)
    low_pts = jnp.arange(low_len, dtype=jnp.int32)
    high_pts = jnp.arange(high_len, dtype=jnp.int32) * low_len
    low_phase = wave_ids[None, :, None] * low_pts[None, None, :] % counts
    high_phase = wave_ids[None, :, None] * high_pts[None, None, :] % counts
    low_angle = 2.0 * jnp.pi * low_phase.astype(jnp.float32) / count_float
    high_angle = 2.0 * jnp.pi * high_phase.astype(jnp.float32) / count_float
    cos_low = jnp.cos(low_angle)[:, :, None, :]
    sin_low = jnp.sin(low_angle)[:, :, None, :]
    cos_high = jnp.cos(high_angle)[:, :, :, None]
    sin_high = jnp.sin(high_angle)[:, :, :, None]
    group_size, wave_total = (cycle_count.shape[0], wave_ids.shape[0])
    cosine = (cos_high * cos_low - sin_high * sin_low).reshape(group_size, wave_total, lon_max)
    sine = (sin_high * cos_low + cos_high * sin_low).reshape(group_size, wave_total, lon_max)
    longitude = jnp.arange(lon_max, dtype=jnp.int32)
    live_mask = (longitude[None, None, :] < counts) & (2 * wave_ids[None, :, None] < counts)
    cosine = jnp.where(live_mask, cosine, 0.0)
    sine_part = jnp.where(live_mask, -sine, 0.0)
    return jnp.stack([cosine, sine_part], axis=1).astype(jnp.bfloat16)


def cycle_trip(fourier, wave_ids, cycle_count, coef_rows):
    wave_total, channels, items, group_size = fourier.shape
    fields = channels // 2
    polys = trig_rows(wave_ids, cycle_count, coef_rows.shape[1])
    factor = jnp.where(wave_ids == 0, 1.0, 2.0).astype(jnp.bfloat16)
    weighted = (fourier * factor[:, None, None, None]).reshape(
        wave_total, 2, fields, items, group_size
    )
    grid_vals = jnp.einsum("mrfig,grmk->gfik", weighted, polys, preferred_element_type=jnp.float32)
    tendency = (grid_vals * (coef_rows[:, None, None, :] + jnp.roll(grid_vals, -1, axis=1))).astype(
        jnp.bfloat16
    )
    analysed = jnp.einsum("gfik,grmk->mrfig", tendency, polys, preferred_element_type=jnp.float32)
    analysed = analysed / cycle_count.astype(jnp.float32)
    return analysed.astype(jnp.bfloat16).reshape(wave_total, channels, items, group_size)


def cycle_group_size():
    for candidate in (8, 4, 2):
        return candidate
    return 1


def damping(depths, own_waves, first, span):
    degree = (own_waves[:, None] + first + jnp.arange(span, dtype=jnp.int32)[None, :]).astype(
        jnp.float32
    )
    return 1.0 / (
        1.0
        + depths[None, :, None] * degree[:, None, :] * (degree[:, None, :] + 1.0) / float(NT * NT)
    )


def inverse_legendre(spectral, legendre, own_lengths):
    wave_local, channels, lev_local, spec_len = spectral.shape
    half_lat = legendre.shape[1]
    row_total = channels * lev_local
    block_width = min(256, spec_len)

    def inverse_per_wave(column, result):
        coeffs = spectral[column].reshape(row_total, spec_len)
        polys = legendre[column]
        length = own_lengths[column]
        blocks = (length + block_width - 1) // block_width

        def inverse_per_block(block_no, sums_pair):
            offset = block_no * block_width
            segment = lax.dynamic_slice_in_dim(coeffs, offset, block_width, 1)
            poly_block = lax.dynamic_slice_in_dim(polys, offset, block_width, 1)
            position = offset + jnp.arange(block_width, dtype=jnp.int32)
            segment = jnp.where(position[None, :] < length, segment, jnp.zeros_like(segment))
            even_sum, odd_sum = sums_pair
            even_piece = jnp.where(position[None, :] % 2 == 0, segment, jnp.zeros_like(segment))
            odd_piece = jnp.where(position[None, :] % 2 == 1, segment, jnp.zeros_like(segment))
            contract = (((1,), (1,)), ((), ()))
            even_sum = even_sum + lax.dot_general(
                even_piece, poly_block, contract, preferred_element_type=jnp.float32
            )
            odd_sum = odd_sum + lax.dot_general(
                odd_piece, poly_block, contract, preferred_element_type=jnp.float32
            )
            return (even_sum, odd_sum)

        zeros_init = jnp.zeros((row_total, half_lat), jnp.float32)
        even_sum, odd_sum = lax.fori_loop(0, blocks, inverse_per_block, (zeros_init, zeros_init))
        northern = even_sum + odd_sum
        southern = jnp.flip(even_sum - odd_sum, axis=1)
        joined = jnp.concatenate([northern, southern], axis=1).astype(jnp.bfloat16)
        return result.at[column].set(joined.reshape(channels, lev_local, 2 * half_lat))

    start_value = jnp.zeros((wave_local, channels, lev_local, 2 * half_lat), jnp.bfloat16)
    return lax.fori_loop(0, wave_local, inverse_per_wave, start_value)


def forward_legendre(returned, legendre, own_lengths, cycle_weights):
    wave_local, channels, lev_local, lat_total = returned.shape
    half_lat = legendre.shape[1]
    spec_len = legendre.shape[2]
    row_total = channels * lev_local
    block_width = min(256, spec_len)
    northern = returned[..., :half_lat].astype(jnp.float32)
    southern = jnp.flip(returned[..., half_lat:], axis=3).astype(jnp.float32)
    even_part = (
        (cycle_weights * (northern + southern))
        .astype(jnp.bfloat16)
        .reshape(wave_local, row_total, half_lat)
    )
    odd_part = (
        (cycle_weights * (northern - southern))
        .astype(jnp.bfloat16)
        .reshape(wave_local, row_total, half_lat)
    )

    def forward_per_wave(column, result):
        polys = legendre[column]
        length = own_lengths[column]
        even_rows = even_part[column]
        odd_rows = odd_part[column]
        blocks = (length + block_width - 1) // block_width

        def forward_per_block(block_no, coeffs):
            offset = block_no * block_width
            poly_block = lax.dynamic_slice_in_dim(polys, offset, block_width, 1)
            position = offset + jnp.arange(block_width, dtype=jnp.int32)
            from_even = jnp.dot(even_rows, poly_block, preferred_element_type=jnp.float32)
            from_odd = jnp.dot(odd_rows, poly_block, preferred_element_type=jnp.float32)
            values = jnp.where(position[None, :] % 2 == 0, from_even, from_odd)
            values = jnp.where(position[None, :] < length, values, 0.0).astype(jnp.bfloat16)
            return lax.dynamic_update_slice_in_dim(coeffs, values, offset, 1)

        coeffs = lax.fori_loop(
            0, blocks, forward_per_block, jnp.zeros((row_total, spec_len), jnp.bfloat16)
        )
        return result.at[column].set(coeffs.reshape(channels, lev_local, spec_len))

    start_value = jnp.zeros((wave_local, channels, lev_local, spec_len), jnp.bfloat16)
    return lax.fori_loop(0, wave_local, forward_per_wave, start_value)


def on_device(
    spectral,
    legendre,
    wave_ids,
    trunc_lengths,
    cycle_points,
    grid_coef,
    cycle_weights,
    modes_in,
    modes_out,
    depths,
):
    wave_rank = lax.axis_index("wave")
    lev_rank = lax.axis_index("lev")
    wave_local, channels, lev_local, spec_len = spectral.shape
    own_waves = lax.dynamic_slice_in_dim(wave_ids, wave_rank * wave_local, wave_local)
    own_lengths = lax.dynamic_slice_in_dim(trunc_lengths, wave_rank * wave_local, wave_local)
    fourier = inverse_legendre(spectral, legendre, own_lengths)
    band_block = lax.all_to_all(fourier, "wave", split_axis=3, concat_axis=0, tiled=True)
    wave_total, chan_count, items, band = band_block.shape
    group_size = cycle_group_size()
    groups = band // group_size
    cycle_count = lax.dynamic_slice_in_dim(cycle_points, wave_rank * band, band)
    stacked = jnp.moveaxis(
        band_block.reshape(wave_total, chan_count, items, groups, group_size), 3, 0
    )
    counts = cycle_count.reshape(groups, group_size)
    coefs = grid_coef.reshape(groups, group_size, grid_coef.shape[1])

    def per_group(packed):
        return cycle_trip(packed[0], wave_ids, packed[1], packed[2])

    results = lax.map(per_group, (stacked, counts, coefs))
    analysed = jnp.moveaxis(results, 0, 3).reshape(wave_total, chan_count, items, band)
    returned = lax.all_to_all(analysed, "wave", split_axis=0, concat_axis=3, tiled=True)
    projected = forward_legendre(returned, legendre, own_lengths, cycle_weights)
    mode_vals = jnp.einsum(
        "kl,mcli->mcki",
        modes_in,
        lax.all_gather(projected, "lev", axis=2, tiled=True),
        preferred_element_type=jnp.float32,
    )
    damp = damping(depths, own_waves, 0, spec_len)
    scaled = (mode_vals * damp[:, None, :, :]).astype(jnp.bfloat16)
    own_rows = lax.dynamic_slice_in_dim(modes_out, lev_rank * lev_local, lev_local, 0)
    update = jnp.einsum(
        "lk,mcki->mcli", own_rows, scaled, preferred_element_type=jnp.float32
    ).astype(jnp.bfloat16)
    return update


def solution(mesh):
    placed = (
        P("wave", None, "lev", None),
        P("wave", None, None),
        P(),
        P(),
        P(),
        P("wave", None),
        P(),
        P(),
        P(),
        P(),
    )
    return jax.shard_map(
        on_device,
        mesh=mesh,
        in_specs=placed,
        out_specs=P("wave", None, "lev", None),
        check_vma=False,
    )
```

profile of v0, /device:TPU:0, one launch (start us, length us, event | category | flops | bytes accessed | tf_op | source)
XLA Modules:
  0.0 746.9 jit_solution(11752609533973577383)
XLA Ops:
  7.4 34.5 %while.138 = (s32[]{:T(128)}, bf16[4,6,16,1280]{3,2,1,0:T(8,128)(2,1)S(1)}, s32[4]{0:T(128)S(1)}, bf16[4,6,16,1280]{3,2,1,0:T(8,128)(2,1)}, bf16[4,640,1280]{2,1...) while((s32[]{:T(128)}, ...), condition=%wide.region_4.5_spmd, body=%wide.region_0.4_spmd.sunk | while | flops 63941424 | bytes 8213980 | solution.py:105
  11.2 6.0 while.142
  41.9 7.7 %copy.30 = bf16[4,6,16,1280]{2,0,1,3:T(4,128)(2,1)} copy(bf16[4,6,16,1280]{3,2,1,0:T(8,128)(2,1)S(1)} %get-tuple-element.681) | data formatting | bytes 1966080 | tf_op jit(solution)/shard_map/while | solution.py:105
  49.6 10.8 %reshape.620 = bf16[8,2,30720]{2,1,0:T(2,128)(2,1)} reshape(bf16[1280,6,4,16]{3,2,1,0:T(4,128)(2,1)} %bitcast.142) | data formatting | bytes 1966080
  60.4 13.9 %all-to-all-start = ((bf16[8,2,30720]{2,1,0:T(2,128)(2,1)}), bf16[8,2,30720]{2,1,0:T(2,128)(2,1)S(1)}, u32[]{:S(2)}, u32[]{:S(2)}) async-start(bf16[8,2,30720]{2,1,0:T(2,128)(2,1)} %reshape.620), calls=%async_computation | async-start | bytes 1966080 | tf_op jit(solution)/shard_map/all_to_all | solution.py:171
  75.2 23.5 %all-to-all-done = bf16[8,2,30720]{2,1,0:T(2,128)(2,1)S(1)} async-done(((bf16[8,2,30720]{2,1,0:T(2,128)(2,1)}), bf16[8,2,30720]{2,1,0:T(2,128)(2,1)S(1)}, u32[]{:S(2)}, u32[]{:S(2)}) %all-to-all-start) | async-done | bytes 983072 | tf_op jit(solution)/shard_map/all_to_all | solution.py:171
  98.7 7.2 reshape.621
  105.9 8.4 %copy.31 = bf16[4,6,16,8,160]{2,4,1,0,3:T(8,128)(2,1)} copy(bf16[4,6,16,8,160]{2,0,1,4,3:T(4,128)(2,1)} %bitcast.143) | data formatting | bytes 1966080 | tf_op jit(solution)/shard_map/all_to_all | solution.py:171
  114.3 9.7 %copy.32 = bf16[20,32,6,16,8]{1,4,3,2,0:T(8,128)(2,1)} copy(bf16[20,32,6,16,8]{3,4,0,2,1:T(8,128)(2,1)} %bitcast.144) | data formatting | bytes 1966080 | tf_op jit(solution)/shard_map/while | solution.py:185
  124.0 488.3 %while.139 = (s32[]{:T(128)}, bf16[20,32,6,16,8]{1,3,2,4,0:T(8,128)(2,1)}, s32[20,8]{1,0:T(8,128)S(1)}, s32[32]{0:T(128)S(1)}, bf16[20,32,6,16,8]{1,4,3,2,0:T(8,128)(2,1)}, /*index=5*/f32[20,8,2560]{2,1,0:T(8,128)}, s32[]{:T(128)}) while((s32[]{:T(128)}, bf16[20,32,6,16,8]{1,3,2,4,0:T(8,128)(2,1)}, s32[20,8]{1,0:T(8,128)S(1)}, ...), condition=%wide.region_6.7_spmd, body=%wide.region_5.6_spmd.sunk | while | flops 270372576 | bytes 39293648 | solution.py:185
  127.9 5.0 multiply_subtract_fusion.2
  152.3 5.0 multiply_subtract_fusion.2
  176.7 5.0 multiply_subtract_fusion.2
  201.1 5.0 multiply_subtract_fusion.2
  225.5 5.0 multiply_subtract_fusion.2
  249.9 5.0 multiply_subtract_fusion.2
  274.3 5.0 multiply_subtract_fusion.2
  298.8 5.0 multiply_subtract_fusion.2
  347.6 5.0 multiply_subtract_fusion.2
  612.3 6.2 copy.34
  622.4 36.0 %all-to-all-done.1 = bf16[32,6,16,160]{3,2,1,0:T(8,128)(2,1)S(1)} async-done(((bf16[32,6,16,160]{3,2,1,0:T(8,128)(2,1)}), bf16[32,6,16,160]{3,2,1,0:T(8,128)(2,1)S(1)}, u32[]{:S(2)}, u32[]{:S(2)}) %all-to-all-start.1) | async-done | bytes 983072 | tf_op jit(solution)/shard_map/all_to_all | solution.py:187
  663.1 31.2 %while.141 = (s32[]{:T(128)}, bf16[4,6,16,1280]{3,2,1,0:T(8,128)(2,1)S(1)}, s32[4]{0:T(128)S(1)}, bf16[4,640,1280]{2,1,0:T(8,128)(2,1)}, bf16[4,96,640]{2,1,0:T(...) while((s32[]{:T(128)}, ...), condition=%wide.region_11.12_spmd, body=%wide.region_7.11_spmd.sunk | while | flops 63090224 | bytes 5803138 | solution.py:150
  667.0 5.5 while.143
  695.8 39.4 %all-gather.2.cloned.1.call-done = bf16[4,6,64,1280]{3,2,1,0:T(8,128)(2,1)} async-done(((bf16[4,6,16,1280]{3,2,1,0:T(8,128)(2,1)}), bf16[4,6,64,1280]{3,2,1,0:T(8,128)(2,1)}) %all-gather.2.cloned.1.call-update) | async-done | bytes 3932176 | tf_op jit(solution)/shard_map/all_gather | solution.py:192
  (643 shorter events, 526.6 us)
Async XLA Ops:
  6.5 728.7 %copy-start = (bf16[64,64]{1,0:T(8,128)(2,1)S(1)}, bf16[64,64]{1,0:T(8,128)(2,1)}, u32[]{:S(2)}) copy-start(bf16[64,64]{1,0:T(8,128)(2,1)} %param.31) | copy-start | bytes 24580
  11.2 6.6 copy-start.3
  23.2 1.8 copy-start.3
  30.3 1.8 copy-start.3
  37.4 3.0 copy-start.3
  60.4 38.3 %all-to-all-start = ((bf16[8,2,30720]{2,1,0:T(2,128)(2,1)}), bf16[8,2,30720]{2,1,0:T(2,128)(2,1)S(1)}, u32[]{:S(2)}, u32[]{:S(2)}) async-start(bf16[8,2,30720]{2,1,0:T(2,128)(2,1)} %reshape.620), calls=%async_computation | async-start | bytes 1966080 | tf_op jit(solution)/shard_map/all_to_all | solution.py:171
  114.3 9.7 %copy-start.2 = (s32[32]{0:T(128)S(1)}, s32[32]{0:T(128)}, u32[]{:S(2)}) copy-start(s32[32]{0:T(128)} %param.26) | copy-start | bytes 388
  618.5 39.9 %all-to-all-start.1 = ((bf16[32,6,16,160]{3,2,1,0:T(8,128)(2,1)}), bf16[32,6,16,160]{3,2,1,0:T(8,128)(2,1)S(1)}, u32[]{:S(2)}, u32[]{:S(2)}) async-start(bf16[32,6,16,160]{3,2,1,0:T(8,128)(2,1)} %copy.34), calls=%async_computation.1 | async-start | bytes 3145728 | tf_op jit(solution)/shard_map/all_to_all | solution.py:187
  622.1 113.1 %all-gather.2.cloned.1.call-start = ((), (), s32[]{:S(2)}) async-start(), calls=%async_computation.2 | async-start | bytes 4915200 | tf_op jit(solution)/shard_map/all_gather | solution.py:192
  659.3 2.5 copy-start.5
  661.0 2.1 copy-start.4
  663.1 32.4 %copy-start.6 = (f32[64]{0:T(128)S(1)}, f32[64]{0:T(128)}, u32[]{:S(2)}) copy-start(f32[64]{0:T(128)} %param.33) | copy-start | bytes 772
  694.3 0.9 copy-start.1
Sparse Core Ops, SparseCore 0:
  695.4 39.8 all-gather.1
where the time goes:
time: 750 us; the launch traced here: 747 us
  local copies, waits for them, and re-layouts  279 us (37%)
  other arithmetic  254 us (34%)
  waiting for transfers between devices  99 us (13%)
  matrix products  75.4 us (10%)
  starting transfers between devices  17.8 us (2%)
  between operations  13.5 us (2%)
  loops' own time  8.18 us (1%)
    sub x20, other arithmetic, trig_rows(): cos_high * cos_low - sin_high * sin_low  99.9 us
    neg x20, local copies, waits for them, and re-layouts, trig_rows(): sine_part = jnp.where(live_mask, -sine, 0.0)  88.2 us
    another operation x32, other arithmetic  55.4 us
    sub x20, local copies, waits for them, and re-layouts, trig_rows(): cos_high * cos_low - sin_high * sin_low  49.5 us
    dot_general x20, matrix products, cycle_trip(): jnp.einsum('gfik,grmk->mrfig', tendency, polys, preferred_element_type=jn...  48 us
    all_gather x1, waiting for transfers between devices, on_device(): lax.all_gather(projected, 'lev', axis=2, tiled=True)  39.4 us
    cos x20, other arithmetic, trig_rows(): cos_low = jnp.cos(low_angle)[:, :, None, :]  36.6 us
    cos x20, other arithmetic, trig_rows(): cos_high = jnp.cos(high_angle)[:, :, :, None]  36.5 us
  transfers between devices with their start and end apart: 3, of which 3 were waited for; matrix products, arithmetic and copies ran while one was open for 0% of the time, Pallas kernels for 0%

commit v1 on v0

v1 whole, which is shorter than its diff:
```python
import jax
import jax.numpy as jnp
from jax import lax
from jax.experimental import pallas as pl
from jax.experimental.pallas import tpu as pltpu
from jax.sharding import PartitionSpec as P

LANES = 128
GROUP = 8
UNROLL = 2
CHUNK = 512


def unit_circle(turns):
    half = jnp.floor(2.0 * turns + 0.5)
    angle = (turns - 0.5 * half) * (2.0 * jnp.pi)
    sign = jnp.where(half == 1.0, -1.0, 1.0)
    sq = angle * angle
    cosine = -1.0 / 3628800.0
    for term in (1.0 / 40320.0, -1.0 / 720.0, 1.0 / 24.0, -0.5, 1.0):
        cosine = cosine * sq + term
    sine = -1.0 / 39916800.0
    for term in (1.0 / 362880.0, -1.0 / 5040.0, 1.0 / 120.0, -1.0 / 6.0, 1.0):
        sine = sine * sq + term
    return cosine * sign, sine * angle * sign


def grid_kernel(pts_ref, inv_ref, flip_ref, wave_ref, coef_ref, weights_ref, out_ref, table, tend):
    waves = wave_ref.shape[0]
    points = coef_ref.shape[1]
    rows = weights_ref.shape[2]
    items = rows // 3
    block = pl.program_id(0)
    wave = wave_ref[...]
    lane = lax.broadcasted_iota(jnp.int32, (1, LANES), 1)
    lane_f = lane.astype(jnp.float32)

    def one(pos, slot):
        pts = pts_ref[block * GROUP + pos]
        pts_f = pts.astype(jnp.float32)
        inv = inv_ref[block * GROUP + pos]
        prod = wave * lane_f
        left = prod - jnp.floor(prod * inv) * pts_f
        cosine, sine = unit_circle(left * inv)
        live = jnp.where(2.0 * wave < pts_f, 1.0, 0.0)
        mid_c = cosine[:, LANES // 2:LANES // 2 + 1]
        mid_s = sine[:, LANES // 2:LANES // 2 + 1]
        step_c = jnp.broadcast_to(1.0 - 2.0 * mid_s * mid_s, (waves, LANES))
        step_s = jnp.broadcast_to(2.0 * mid_s * mid_c, (waves, LANES))
        cosine = cosine * live
        sine = -sine * live
        for hi in range(points // LANES):
            table[slot, 0:waves, hi * LANES:(hi + 1) * LANES] = cosine.astype(jnp.bfloat16)
            table[slot, waves:2 * waves, hi * LANES:(hi + 1) * LANES] = sine.astype(jnp.bfloat16)
            cosine, sine = (
                cosine * step_c + sine * step_s,
                sine * step_c - cosine * step_s,
            )
        row = jnp.where(flip_ref[0] == 1, GROUP - 1 - pos, pos)
        weights = weights_ref[pos]
        for start in range(0, points, CHUNK):
            cols = slice(start, start + CHUNK)
            grid = lax.dot_general(
                weights, table[slot, :, cols], (((0,), (0,)), ((), ())),
                preferred_element_type=jnp.float32,
            )
            coef = coef_ref[pl.ds(row, 1), cols]
            rolled = jnp.concatenate([grid[items:], grid[:items]], axis=0)
            col_id = start + lax.broadcasted_iota(jnp.int32, (1, CHUNK), 1)
            value = jnp.where(col_id < pts, grid * (coef + rolled), 0.0)
            tend[slot, :, cols] = value.astype(jnp.bfloat16)
        back = lax.dot_general(
            table[slot], tend[slot], (((1,), (1,)), ((), ())),
            preferred_element_type=jnp.float32,
        )
        out_ref[pos] = (back * inv).astype(jnp.bfloat16)

    def step(index, carry):
        for slot in range(UNROLL):
            one(index * UNROLL + slot, slot)
        return carry

    lax.fori_loop(0, GROUP // UNROLL, step, 0)


def grid_trip(weights, wave_ids, counts, flip, coefs):
    band, modes, rows = weights.shape
    waves = wave_ids.shape[0]
    points = coefs.shape[1]
    blocks = band // GROUP
    wave_f = jnp.broadcast_to(wave_ids.astype(jnp.float32)[:, None], (waves, LANES))
    spec = pltpu.PrefetchScalarGridSpec(
        num_scalar_prefetch=3,
        grid=(blocks,),
        in_specs=[
            pl.BlockSpec((waves, LANES), lambda b, p, v, f: (0, 0)),
            pl.BlockSpec(
                (GROUP, points), lambda b, p, v, f: (jnp.where(f[0] == 1, blocks - 1 - b, b), 0)
            ),
            pl.BlockSpec((GROUP, modes, rows), lambda b, p, v, f: (b, 0, 0)),
        ],
        out_specs=pl.BlockSpec((GROUP, modes, rows), lambda b, p, v, f: (b, 0, 0)),
        scratch_shapes=[
            pltpu.VMEM((UNROLL, modes, points), jnp.bfloat16),
            pltpu.VMEM((UNROLL, rows, points), jnp.bfloat16),
        ],
    )
    return pl.pallas_call(
        grid_kernel,
        grid_spec=spec,
        out_shape=jax.ShapeDtypeStruct((band, modes, rows), jnp.bfloat16),
        compiler_params=pltpu.CompilerParams(dimension_semantics=("arbitrary",)),
    )(counts, 1.0 / counts.astype(jnp.float32), flip, wave_f, coefs, weights)


def on_device(
    spectral,
    legendre,
    wave_ids,
    trunc_lengths,
    cycle_points,
    grid_coef,
    cycle_weights,
    modes_in,
    modes_out,
    depths,
):
    wave_size = lax.axis_size("wave")
    lev_size = lax.axis_size("lev")
    wave_rank = lax.axis_index("wave")
    lev_rank = lax.axis_index("lev")
    wave_local, channels, lev_local, spec_len = spectral.shape
    half_lat = legendre.shape[1]
    wave_total = wave_ids.shape[0]
    fields = channels // 2
    levels = lev_local * lev_size
    items = channels * lev_local
    band = 2 * half_lat // wave_size
    north_bands = wave_size // 2
    own_waves = lax.dynamic_slice_in_dim(wave_ids, wave_rank * wave_local, wave_local)
    own_lengths = lax.dynamic_slice_in_dim(trunc_lengths, wave_rank * wave_local, wave_local)
    position = jnp.arange(spec_len, dtype=jnp.int32)

    factor = jnp.where(own_waves == 0, 1.0, 2.0).astype(jnp.bfloat16)
    live = (position[None, :] < own_lengths[:, None])[:, None, :]
    flat = spectral.reshape(wave_local, items, spec_len) * factor[:, None, None]
    zero = jnp.zeros_like(flat)
    even_in = jnp.where(live & (position % 2 == 0), flat, zero)
    odd_in = jnp.where(live & (position % 2 == 1), flat, zero)
    both = jnp.concatenate([even_in, odd_in], axis=1)
    sums = jnp.einsum("mji,mri->mjr", legendre, both, preferred_element_type=jnp.float32)
    even_sum, odd_sum = sums[..., :items], sums[..., items:]
    north = (even_sum + odd_sum).astype(jnp.bfloat16)
    south = (even_sum - odd_sum).astype(jnp.bfloat16)

    def banded(part):
        return jnp.swapaxes(part, 0, 1).reshape(north_bands, band, wave_local * items)

    blocks = jnp.concatenate([banded(north), banded(south)[::-1]], axis=0)
    got = lax.all_to_all(blocks, "wave", split_axis=0, concat_axis=0, tiled=True)
    weights = got.reshape(wave_size, band, wave_local, 2, fields * lev_local)
    weights = weights.transpose(1, 3, 0, 2, 4).reshape(band, 2 * wave_total, fields * lev_local)

    flip = wave_rank >= north_bands
    north_rank = jnp.where(flip, wave_size - 1 - wave_rank, wave_rank)
    counts = lax.dynamic_slice_in_dim(cycle_points, north_rank * band, band)
    analysed = grid_trip(weights, wave_ids, counts, flip.astype(jnp.int32)[None], grid_coef)

    share = wave_local * channels // lev_size
    per_wave = channels // share
    sent = analysed.reshape(band, 2, wave_total, fields, lev_local)
    sent = sent.transpose(2, 1, 3, 0, 4)
    sent = sent.reshape(wave_size * lev_size, share, band, lev_local)
    back = lax.all_to_all(sent, ("wave", "lev"), split_axis=0, concat_axis=0, tiled=True)
    back = back.reshape(2, north_bands, lev_size, share, band, lev_local)
    northern = back[0].astype(jnp.float32)
    southern = back[1][::-1].astype(jnp.float32)
    scale = cycle_weights.reshape(north_bands, 1, 1, band, 1)
    even = (scale * (northern + southern)).astype(jnp.bfloat16)
    odd = (scale * (northern - southern)).astype(jnp.bfloat16)
    parts = jnp.stack([even, odd])
    parts = parts.transpose(0, 3, 2, 5, 1, 4).reshape(2, share * levels, half_lat)
    column = lev_rank // per_wave
    own_polys = lax.dynamic_index_in_dim(legendre, column, 0, keepdims=False)
    own_wave = lax.dynamic_index_in_dim(own_waves, column, 0, keepdims=False)
    own_length = lax.dynamic_index_in_dim(own_lengths, column, 0, keepdims=False)
    both_out = jnp.einsum("erj,ji->eri", parts, own_polys, preferred_element_type=jnp.float32)
    projected = jnp.where(position % 2 == 0, both_out[0], both_out[1])
    projected = jnp.where(position < own_length, projected, 0.0).astype(jnp.bfloat16)
    projected = projected.reshape(share, levels, spec_len)
    mode_vals = jnp.einsum("ql,cli->cqi", modes_in, projected, preferred_element_type=jnp.float32)
    degree = (own_wave + position).astype(jnp.float32)
    damp = 1.0 / (1.0 + depths[:, None] * degree * (degree + 1.0) / float(spec_len * spec_len))
    scaled = (mode_vals * damp).astype(jnp.bfloat16)
    update = jnp.einsum(
        "lq,cqi->cli", modes_out, scaled, preferred_element_type=jnp.float32
    ).astype(jnp.bfloat16)
    update = lax.all_to_all(update, "lev", split_axis=1, concat_axis=0, tiled=True)
    return update.reshape(wave_local, channels, lev_local, spec_len)


def solution(mesh):
    placed = (
        P("wave", None, "lev", None),
        P("wave", None, None),
        P(),
        P(),
        P(),
        P("wave", None),
        P(),
        P(),
        P(),
        P(),
    )
    return jax.shard_map(
        on_device,
        mesh=mesh,
        in_specs=placed,
        out_specs=P("wave", None, "lev", None),
        check_vma=False,
    )
```

time: 750 us -> 181 us (0.24)
  local copies, waits for them, and re-layouts: 279 us -> 19.6 us
  other arithmetic: 254 us -> 7.71 us
  matrix products: 75.4 us -> 8.94 us
  Pallas kernels: 0 us -> 56.2 us
  waiting for transfers between devices: 99 us -> 57.1 us
  blocking collectives: 0 us -> 19.7 us
  between operations: 13.5 us -> 0.25 us
  loops' own time: 8.18 us -> 0 us
    sub x24 -> x0, other arithmetic: 100 us -> none  [the longest x20 99.9 us: trig_rows(): cos_high * cos_low - sin_high * sin_low]
    neg x20 -> x0, local copies, waits for them, and re-layouts: 88.2 us -> none  [trig_rows(): sine_part = jnp.where(live_mask, -sine, 0.0)]
    cos x40 -> x0, other arithmetic: 73.1 us -> none  [the longest x20 36.6 us: trig_rows(): cos_low = jnp.cos(low_angle)[:, :, None, :]]
    dot_general x77 -> x3, matrix products: 75.4 us -> 8.94 us  [the longest x1 5.09 us: on_device(): jnp.einsum('mji,mri->mjr', legendre, both, preferred_element_type=jnp.flo...]
    pallas_call x0 -> x1, Pallas kernels: none -> 56.2 us  [grid_trip(): pl.pallas_call(grid_kernel, grid_spec=spec, out_shape=jax.ShapeDtypeStruc...]
    another operation x32 -> x1, other arithmetic: 55.4 us -> 0.46 us  [on_device(): parts = jnp.stack([even, odd])]
    sub x20 -> x0, local copies, waits for them, and re-layouts: 49.5 us -> none  [trig_rows(): cos_high * cos_low - sin_high * sin_low]
    all_gather x1 -> x0, waiting for transfers between devices: 39.4 us -> none  [on_device(): lax.all_gather(projected, 'lev', axis=2, tiled=True)]
  transfers between devices with their start and end apart: 3 -> 2, of which waited for: 3 -> 2; matrix products, arithmetic and copies ran while one was open for 0% -> 3% of each run, Pallas kernels for 0% -> 0%
where the time goes in v1:
time: 181 us; the launch traced here: 180 us
  waiting for transfers between devices  57.1 us (32%)
  Pallas kernels  56.2 us (31%)
  blocking collectives  19.7 us (11%)
  local copies, waits for them, and re-layouts  19.6 us (11%)
  starting transfers between devices  10.9 us (6%)
  matrix products  8.94 us (5%)
  other arithmetic  7.71 us (4%)
    pallas_call x1, Pallas kernels, grid_trip(): pl.pallas_call(grid_kernel, grid_spec=spec, out_shape=jax.ShapeDtypeStruc...  56.2 us
    all_to_all x1, waiting for transfers between devices, on_device(): lax.all_to_all(sent, ('wave', 'lev'), split_axis=0, concat_axis=0, tiled=...  34.1 us
    all_to_all x1, waiting for transfers between devices, on_device(): lax.all_to_all(blocks, 'wave', split_axis=0, concat_axis=0, tiled=True)  23 us
    all_to_all x1, blocking collectives, on_device(): lax.all_to_all(update, 'lev', split_axis=1, concat_axis=0, tiled=True)  19.7 us
    all_to_all x1, starting transfers between devices, on_device(): lax.all_to_all(blocks, 'wave', split_axis=0, concat_axis=0, tiled=True)  7.31 us
    dot_general x1, matrix products, on_device(): jnp.einsum('mji,mri->mjr', legendre, both, preferred_element_type=jnp.flo...  5.09 us
    pallas_call x1, local copies, waits for them, and re-layouts, grid_trip(): pl.pallas_call(grid_kernel, grid_spec=spec, out_shape=jax.ShapeDtypeStruc...  3.72 us
    transpose x1, local copies, waits for them, and re-layouts, on_device(): weights.transpose(1, 3, 0, 2, 4)  3.72 us
  transfers between devices with their start and end apart: 2, of which 2 were waited for; matrix products, arithmetic and copies ran while one was open for 3% of the time, Pallas kernels for 0%

profile of v1, /device:TPU:0, one launch (start us, length us, event | category | flops | bytes accessed | tf_op | source)
XLA Modules:
  0.0 180.4 jit_solution(8033903747674170540)
XLA Ops:
  0.0 0.7 dynamic_slice.25
  0.7 0.7 fusion.38
  1.6 1.4 broadcast_select_fusion.1
  3.0 5.1 %fusion.10 = f32[4,640,192]{1,2,0:T(8,128)S(1)} fusion(bf16[4,640,1280]{2,1,0:T(8,128)(2,1)} %param.11, bf16[4,96,1280]{2,1,0:T(8,128)(2,1)S(1)} %get-tuple-element.16, bf16[4,96,1280]{2,1,0:T(8,128)(2,1)S(1)} %get-tuple-element.15), kind=kOutput, calls=%fused_computation.15 | convolution fusion | flops 1262223360 | bytes 10485760 | tf_op jit(solution)/shard_map/mji,mri->mjr/dot_general | solution.py:151
  8.3 0.9 copy.21
  9.6 0.9 copy.20
  11.0 1.1 pad_maximum_fusion
  12.0 7.3 %all-to-all-start = ((bf16[8,160,384]{2,1,0:T(8,128)(2,1)}), bf16[8,160,384]{2,1,0:T(8,128)(2,1)S(1)}, u32[]{:S(2)}, u32[]{:S(2)}) async-start(bf16[8,160,384]{2,1,0:T(8,128)(2,1)} %pad_maximum_fusion), calls=%async_computation | async-start | bytes 1966080 | tf_op jit(solution)/shard_map/all_to_all | solution.py:160
  19.4 1.3 convert_divide_fusion
  20.7 23.0 %all-to-all-done = bf16[8,160,384]{2,1,0:T(8,128)(2,1)S(1)} async-done(((bf16[8,160,384]{2,1,0:T(8,128)(2,1)}), bf16[8,160,384]{2,1,0:T(8,128)(2,1)S(1)}, u32[]{:S(2)}, u32[]{:S(2)}) %all-to-all-start) | async-done | bytes 983072 | tf_op jit(solution)/shard_map/all_to_all | solution.py:160
  43.7 0.7 copy.22
  44.4 3.7 %copy.23 = bf16[160,2,8,4,48]{4,3,2,1,0:T(4,128)(2,1)} copy(bf16[160,2,8,4,48]{0,4,1,3,2:T(8,128)(2,1)S(1)} %bitcast.62) | data formatting | bytes 1966080 | tf_op jit(solution)/shard_map/transpose | solution.py:162
  48.8 56.2 %shard_map.100 = bf16[160,64,48]{2,1,0:T(8,128)(2,1)} custom-call(s32[160]{0:T(256)} %get-tuple-element.6.pts_ref, f32[160]{0:T(256)} %get-tuple-element.5.inv_ref, s32[1]{0:T(128)} %bitcast.1.flip_ref, f32[32,128]{1,0:T(8,128)} %broadcast_in_dim.61.wave_ref, f32[160,2560]{1,0:T(8,128)} %coef_ref.1, bf16[160,64,48]{2,1,0:T(8,128)(2,1)} %bitcast.61), custom_call_target="tpu_custom_call" | custom-call | tf_op jit(solution)/shard_map/pallas_call | solution.py:108
  105.0 3.7 %copy.24 = bf16[160,64,48]{0,2,1:T(8,128)(2,1)S(1)} copy(bf16[160,64,48]{2,1,0:T(8,128)(2,1)} %shard_map.100) | data formatting | bytes 1966080 | tf_op jit(solution)/shard_map/pallas_call | solution.py:108
  108.7 1.4 copy.25
  110.1 3.6 %all-to-all-start.1 = ((bf16[32,6,160,16]{2,3,1,0:T(8,128)(2,1)}), bf16[32,6,160,16]{2,3,1,0:T(8,128)(2,1)S(1)}, u32[]{:S(2)}, u32[]{:S(2)}) async-start(bf16[32,6,160,16]{2,3,1,0:T(8,128)(2,1)} %bitcast.11), calls=%async_computation.1 | async-start | bytes 3145728 | tf_op jit(solution)/shard_map/all_to_all | solution.py:174
  115.1 0.7 iota_compare_fusion.1
  117.2 34.1 %all-to-all-done.1 = bf16[32,6,160,16]{2,3,1,0:T(8,128)(2,1)S(1)} async-done(((bf16[32,6,160,16]{2,3,1,0:T(8,128)(2,1)}), bf16[32,6,160,16]{2,3,1,0:T(8,128)(2,1)S(1)}, u32[]{:S(2)}, u32[]{:S(2)}) %all-to-all-start.1) | async-done | bytes 983072 | tf_op jit(solution)/shard_map/all_to_all | solution.py:174
  152.2 1.2 copy.26
  153.5 1.0 reshape.182
  154.5 3.1 %fusion.7 = bf16[2,384,1280]{2,1,0:T(8,128)(2,1)S(1)} fusion(bf16[2,384,640]{2,1,0:T(8,128)(2,1)S(1)} %reshape.182, bf16[4,640,1280]{2,1,0:T(8,128)(2,1)} %param.11, s32[]{:T(128)S(6)} %select_n.66), kind=kOutput, calls=%fused_computation.12 | convolution fusion | flops 1258291200 | bytes 4587524 | tf_op jit(solution)/shard_map/erj,ji->eri/dot_general | solution.py:187
  158.3 0.7 fusion.2
  159.6 19.7 %all_to_all.25 = bf16[6,64,1280]{2,0,1:T(8,128)(2,1)S(1)} all-to-all(bf16[6,64,1280]{2,0,1:T(8,128)(2,1)S(1)} %copy.27), channel_id=1, replica_groups=mesh['wave'=8,'lev'=4] {'lev'}, dimensions={1} | all-to-all | bytes 1966080 | tf_op jit(solution)/shard_map/all_to_all | solution.py:198
  179.3 1.1 copy.30
  (31 shorter events, 6.8 us)
Async XLA Ops:
  0.0 157.8 %copy-start = (bf16[64,64]{1,0:T(8,128)(2,1)S(1)}, bf16[64,64]{1,0:T(8,128)(2,1)}, u32[]{:S(2)}) copy-start(bf16[64,64]{1,0:T(8,128)(2,1)} %param.18) | copy-start | bytes 24580
  11.0 8.4 %copy-start.4 = (s32[32]{0:T(128)S(1)}, s32[32]{0:T(128)}, u32[]{:S(2)}) copy-start(s32[32]{0:T(128)} %param.12) | copy-start | bytes 388
  12.0 31.7 %all-to-all-start = ((bf16[8,160,384]{2,1,0:T(8,128)(2,1)}), bf16[8,160,384]{2,1,0:T(8,128)(2,1)S(1)}, u32[]{:S(2)}, u32[]{:S(2)}) async-start(bf16[8,160,384]{2,1,0:T(8,128)(2,1)} %pad_maximum_fusion), calls=%async_computation | async-start | bytes 1966080 | tf_op jit(solution)/shard_map/all_to_all | solution.py:160
  110.1 4.2 %copy-start.5 = (s32[32]{0:T(128)S(1)}, s32[32]{0:T(128)}, u32[]{:S(2)}) copy-start(s32[32]{0:T(128)} %param.13) | copy-start | bytes 388
  110.1 4.9 %copy-start.1 = (f32[640]{0:T(1024)S(1)}, f32[640]{0:T(1024)}, u32[]{:S(2)}) copy-start(f32[640]{0:T(1024)} %param.16) | copy-start | bytes 7684
  110.1 7.0 %copy-start.2 = (f32[64]{0:T(128)S(1)}, f32[64]{0:T(128)}, u32[]{:S(2)}) copy-start(f32[64]{0:T(128)} %param.19) | copy-start | bytes 772
  110.1 41.2 %all-to-all-start.1 = ((bf16[32,6,160,16]{2,3,1,0:T(8,128)(2,1)}), bf16[32,6,160,16]{2,3,1,0:T(8,128)(2,1)S(1)}, u32[]{:S(2)}, u32[]{:S(2)}) async-start(bf16[32,6,160,16]{2,3,1,0:T(8,128)(2,1)} %bitcast.11), calls=%async_computation.1 | async-start | bytes 3145728 | tf_op jit(solution)/shard_map/all_to_all | solution.py:174
  157.6 0.7 copy-start.3

commit v2 on v1

v2 whole, which is shorter than its diff:
```python
import functools

import jax
import jax.numpy as jnp
from jax import lax
from jax.experimental import pallas as pl
from jax.experimental.pallas import tpu as pltpu
from jax.sharding import PartitionSpec as P

LANES = 128
UNROLL = 2
CHUNK = 512


def unit_circle(turns):
    half = jnp.floor(2.0 * turns + 0.5)
    angle = (turns - 0.5 * half) * (2.0 * jnp.pi)
    sign = jnp.where(half == 1.0, -1.0, 1.0)
    sq = angle * angle
    cosine = -1.0 / 3628800.0
    for term in (1.0 / 40320.0, -1.0 / 720.0, 1.0 / 24.0, -0.5, 1.0):
        cosine = cosine * sq + term
    sine = -1.0 / 39916800.0
    for term in (1.0 / 362880.0, -1.0 / 5040.0, 1.0 / 120.0, -1.0 / 6.0, 1.0):
        sine = sine * sq + term
    return cosine * sign, sine * angle * sign


def grid_kernel(pts_ref, inv_ref, wave_ref, coef_ref, weights_ref, out_ref, table, tend, *, items):
    waves = wave_ref.shape[0]
    points = coef_ref.shape[1]
    rows = weights_ref.shape[2]
    wave = wave_ref[...]
    lane = lax.broadcasted_iota(jnp.int32, (1, LANES), 1)
    lane_f = lane.astype(jnp.float32)

    def one(pos, slot):
        pts = pts_ref[pos]
        pts_f = pts.astype(jnp.float32)
        inv = inv_ref[pos]
        prod = wave * lane_f
        left = prod - jnp.floor(prod * inv) * pts_f
        cosine, sine = unit_circle(left * inv)
        live = jnp.where(2.0 * wave < pts_f, 1.0, 0.0)
        mid_c = cosine[:, LANES // 2:LANES // 2 + 1]
        mid_s = sine[:, LANES // 2:LANES // 2 + 1]
        step_c = jnp.broadcast_to(1.0 - 2.0 * mid_s * mid_s, (waves, LANES))
        step_s = jnp.broadcast_to(2.0 * mid_s * mid_c, (waves, LANES))
        cosine = cosine * live
        sine = -sine * live
        for hi in range(points // LANES):
            inside = hi * LANES + lane < pts
            cols = slice(hi * LANES, (hi + 1) * LANES)
            table[slot, 0:waves, cols] = jnp.where(inside, cosine, 0.0).astype(jnp.bfloat16)
            table[slot, waves:2 * waves, cols] = jnp.where(inside, sine, 0.0).astype(jnp.bfloat16)
            cosine, sine = (
                cosine * step_c + sine * step_s,
                sine * step_c - cosine * step_s,
            )
        weights = weights_ref[pos]
        for start in range(0, points, CHUNK):
            cols = slice(start, start + CHUNK)
            grid = lax.dot_general(
                weights, table[slot, :, cols], (((0,), (0,)), ((), ())),
                preferred_element_type=jnp.float32,
            )
            coef = coef_ref[pl.ds(pos, 1), cols]
            for first in range(0, rows, 3 * items):
                parts = [grid[first + f * items:first + (f + 1) * items] for f in range(3)]
                for f in range(3):
                    value = parts[f] * (coef + parts[(f + 1) % 3])
                    low = first + f * items
                    tend[slot, low:low + items, cols] = value.astype(jnp.bfloat16)
        back = lax.dot_general(
            table[slot], tend[slot], (((1,), (1,)), ((), ())),
            preferred_element_type=jnp.float32,
        )
        out_ref[pos] = (back * inv).astype(jnp.bfloat16)

    count = coef_ref.shape[0]
    together = UNROLL if count % UNROLL == 0 else 1

    def step(index, carry):
        for slot in range(together):
            one(index * together + slot, slot)
        return carry

    lax.fori_loop(0, count // together, step, 0)


def grid_trip(weights, wave_ids, counts, coefs, items):
    count, modes, rows = weights.shape
    waves = wave_ids.shape[0]
    points = coefs.shape[1]
    wave_f = jnp.broadcast_to(wave_ids.astype(jnp.float32)[:, None], (waves, LANES))
    smem = pl.BlockSpec(memory_space=pltpu.SMEM)
    vmem = pl.BlockSpec(memory_space=pltpu.VMEM)
    return pl.pallas_call(
        functools.partial(grid_kernel, items=items),
        in_specs=[smem, smem, vmem, vmem, vmem],
        out_specs=vmem,
        out_shape=jax.ShapeDtypeStruct((count, modes, rows), jnp.bfloat16),
        scratch_shapes=[
            pltpu.VMEM((UNROLL, modes, points), jnp.bfloat16),
            pltpu.VMEM((UNROLL, rows, points), jnp.bfloat16),
        ],
    )(counts, 1.0 / counts.astype(jnp.float32), wave_f, coefs, weights)


def on_device(
    spectral,
    legendre,
    wave_ids,
    trunc_lengths,
    cycle_points,
    grid_coef,
    cycle_weights,
    modes_in,
    modes_out,
    depths,
):
    wave_size = lax.axis_size("wave")
    lev_size = lax.axis_size("lev")
    wave_rank = lax.axis_index("wave")
    lev_rank = lax.axis_index("lev")
    wave_local, channels, lev_local, spec_len = spectral.shape
    half_lat = legendre.shape[1]
    wave_total = wave_ids.shape[0]
    fields = channels // 2
    levels = lev_local * lev_size
    items = channels * lev_local
    everyone = wave_size * lev_size
    band = 2 * half_lat // wave_size
    sub = band // lev_size
    north_bands = wave_size // 2
    own_waves = lax.dynamic_slice_in_dim(wave_ids, wave_rank * wave_local, wave_local)
    own_lengths = lax.dynamic_slice_in_dim(trunc_lengths, wave_rank * wave_local, wave_local)
    position = jnp.arange(spec_len, dtype=jnp.int32)

    flip = wave_rank >= north_bands
    north_rank = jnp.where(flip, wave_size - 1 - wave_rank, wave_rank)
    counts = lax.dynamic_slice_in_dim(cycle_points, north_rank * band + lev_rank * sub, sub)
    coef_row = jnp.where(flip, band - (lev_rank + 1) * sub, lev_rank * sub)
    coefs = lax.dynamic_slice_in_dim(grid_coef, coef_row, sub, 0)
    coefs = jnp.where(flip, coefs[::-1], coefs)

    factor = jnp.where(own_waves == 0, 1.0, 2.0).astype(jnp.bfloat16)
    live = (position[None, :] < own_lengths[:, None])[:, None, :]
    flat = spectral.reshape(wave_local, items, spec_len) * factor[:, None, None]
    zero = jnp.zeros_like(flat)
    even_in = jnp.where(live & (position % 2 == 0), flat, zero)
    odd_in = jnp.where(live & (position % 2 == 1), flat, zero)
    both = jnp.concatenate([even_in, odd_in], axis=1)
    sums = jnp.einsum("mji,mri->mjr", legendre, both, preferred_element_type=jnp.float32)
    even_sum, odd_sum = sums[..., :items], sums[..., items:]
    north = (even_sum + odd_sum).astype(jnp.bfloat16)
    south = (even_sum - odd_sum).astype(jnp.bfloat16)

    def banded(part):
        rows = jnp.swapaxes(part, 0, 1)
        return rows.reshape(north_bands, lev_size, sub, wave_local * items)

    blocks = jnp.concatenate([banded(north), banded(south)[::-1]], axis=0)
    blocks = blocks.reshape(everyone, sub, wave_local * items)

    share = wave_local * channels // lev_size
    parts_of_r = share // fields
    first = sub // 16 * 8
    cuts = [(0, first), (first, sub)] if sub % 8 == 0 and first else [(0, sub)]
    pieces = []
    for low, high in cuts:
        size = high - low
        got = lax.all_to_all(
            blocks[:, low:high], ("wave", "lev"), split_axis=0, concat_axis=0, tiled=True
        )
        weights = got.reshape(wave_size, lev_size, size, wave_local, 2, fields * lev_local)
        weights = weights.transpose(2, 4, 0, 3, 1, 5)
        weights = weights.reshape(size, 2 * wave_total, fields * levels)
        analysed = grid_trip(weights, wave_ids, counts[low:high], coefs[low:high], lev_local)
        sent = analysed.reshape(size, 2 // parts_of_r, parts_of_r, wave_total, fields * levels)
        sent = sent.transpose(3, 1, 0, 2, 4).reshape(everyone, size, share * levels)
        pieces.append(
            lax.all_to_all(sent, ("wave", "lev"), split_axis=0, concat_axis=0, tiled=True)
        )
    back = jnp.concatenate(pieces, axis=1) if len(pieces) > 1 else pieces[0]
    back = back.reshape(2, north_bands, band, share * levels)
    northern = back[0].reshape(half_lat, share * levels).astype(jnp.float32)
    southern = back[1][::-1].reshape(half_lat, share * levels).astype(jnp.float32)
    scale = cycle_weights[:, None]
    even = (scale * (northern + southern)).astype(jnp.bfloat16)
    odd = (scale * (northern - southern)).astype(jnp.bfloat16)
    per_wave = channels // share
    column = lev_rank // per_wave
    own_polys = lax.dynamic_index_in_dim(legendre, column, 0, keepdims=False)
    own_wave = lax.dynamic_index_in_dim(own_waves, column, 0, keepdims=False)
    own_length = lax.dynamic_index_in_dim(own_lengths, column, 0, keepdims=False)
    from_even = jnp.einsum("jr,ji->ri", even, own_polys, preferred_element_type=jnp.float32)
    from_odd = jnp.einsum("jr,ji->ri", odd, own_polys, preferred_element_type=jnp.float32)
    projected = jnp.where(position % 2 == 0, from_even, from_odd)
    projected = jnp.where(position < own_length, projected, 0.0).astype(jnp.bfloat16)
    projected = projected.reshape(parts_of_r, lev_size, fields, lev_local, spec_len)
    projected = projected.transpose(0, 2, 1, 3, 4).reshape(share, levels, spec_len)
    mode_vals = jnp.einsum("ql,cli->cqi", modes_in, projected, preferred_element_type=jnp.float32)
    degree = (own_wave + position).astype(jnp.float32)
    damp = 1.0 / (1.0 + depths[:, None] * degree * (degree + 1.0) / float(spec_len * spec_len))
    scaled = (mode_vals * damp).astype(jnp.bfloat16)
    update = jnp.einsum(
        "lq,cqi->cli", modes_out, scaled, preferred_element_type=jnp.float32
    ).astype(jnp.bfloat16)
    update = lax.all_to_all(update, "lev", split_axis=1, concat_axis=0, tiled=True)
    return update.reshape(wave_local, channels, lev_local, spec_len)


def solution(mesh):
    placed = (
        P("wave", None, "lev", None),
        P("wave", None, None),
        P(),
        P(),
        P(),
        P("wave", None),
        P(),
        P(),
        P(),
        P(),
    )
    return jax.shard_map(
        on_device,
        mesh=mesh,
        in_specs=placed,
        out_specs=P("wave", None, "lev", None),
        check_vma=False,
    )
```

time: 181 us -> 147 us (0.81)
  waiting for transfers between devices: 57.1 us -> 25.7 us
  Pallas kernels: 56.2 us -> 33.8 us
  starting transfers between devices: 10.9 us -> 21.6 us
  local copies, waits for them, and re-layouts: 19.6 us -> 27 us
    pallas_call x1 -> x2, Pallas kernels: 56.2 us -> 33.8 us  [grid_trip(): pl.pallas_call(functools.partial(grid_kernel, items=items), in_specs=[sme...]
    all_to_all x1 -> x2, waiting for transfers between devices: 34.1 us -> 13.3 us  [on_device(): lax.all_to_all(sent, ('wave', 'lev'), split_axis=0, concat_axis=0, tiled=...]
    all_to_all x1 -> x2, waiting for transfers between devices: 23 us -> 12.4 us  [on_device(): lax.all_to_all(blocks[:, low:high], ('wave', 'lev'), split_axis=0, concat...]
    reshape x3 -> x11, local copies, waits for them, and re-layouts: 1.88 us -> 12 us  [the longest x2 3.57 us: on_device(): analysed.reshape(size, 2 // parts_of_r, parts_of_r, wave_total, fields *...]
    all_to_all x1 -> x2, starting transfers between devices: 3.59 us -> 11.7 us  [on_device(): lax.all_to_all(sent, ('wave', 'lev'), split_axis=0, concat_axis=0, tiled=...]
    transpose x5 -> x4, local copies, waits for them, and re-layouts: 8.05 us -> 3.75 us  [the longest x2 2.03 us: on_device(): weights = weights.transpose(2, 4, 0, 3, 1, 5)]
    pallas_call x1 -> x0, local copies, waits for them, and re-layouts: 3.72 us -> none  [grid_trip(): pl.pallas_call(grid_kernel, grid_spec=spec, out_shape=jax.ShapeDtypeStruc...]
    slice x2 -> x6, local copies, waits for them, and re-layouts: 0.23 us -> 3.77 us  [the longest x2 1.66 us: on_device(): blocks[:, low:high]]
  transfers between devices with their start and end apart: 2 -> 4, of which waited for: 2 -> 2; matrix products, arithmetic and copies ran while one was open for 3% -> 17% of each run, Pallas kernels for 0% -> 23%
where the time goes in v2:
time: 147 us; the launch traced here: 146 us
  Pallas kernels  33.8 us (23%)
  local copies, waits for them, and re-layouts  27 us (18%)
  waiting for transfers between devices  25.7 us (17%)
  starting transfers between devices  21.6 us (15%)
  blocking collectives  19.7 us (13%)
  matrix products  10.6 us (7%)
  other arithmetic  7.08 us (5%)
    pallas_call x2, Pallas kernels, grid_trip(): pl.pallas_call(functools.partial(grid_kernel, items=items), in_specs=[sme...  33.8 us
    all_to_all x1, blocking collectives, on_device(): lax.all_to_all(update, 'lev', split_axis=1, concat_axis=0, tiled=True)  19.7 us
    all_to_all x2, waiting for transfers between devices, on_device(): lax.all_to_all(sent, ('wave', 'lev'), split_axis=0, concat_axis=0, tiled=...  13.3 us
    all_to_all x2, waiting for transfers between devices, on_device(): lax.all_to_all(blocks[:, low:high], ('wave', 'lev'), split_axis=0, concat...  12.4 us
    all_to_all x2, starting transfers between devices, on_device(): lax.all_to_all(sent, ('wave', 'lev'), split_axis=0, concat_axis=0, tiled=...  11.7 us
    all_to_all x2, starting transfers between devices, on_device(): lax.all_to_all(blocks[:, low:high], ('wave', 'lev'), split_axis=0, concat...  9.94 us
    dot_general x1, matrix products, on_device(): jnp.einsum('mji,mri->mjr', legendre, both, preferred_element_type=jnp.flo...  5.09 us
    reshape x2, local copies, waits for them, and re-layouts, on_device(): analysed.reshape(size, 2 // parts_of_r, parts_of_r, wave_total, fields *...  3.57 us
  transfers between devices with their start and end apart: 4, of which 2 were waited for; matrix products, arithmetic and copies ran while one was open for 17% of the time, Pallas kernels for 23%

profile of v2, /device:TPU:0, one launch (start us, length us, event | category | flops | bytes accessed | tf_op | source)
XLA Modules:
  0.0 145.8 jit_solution(6439329253124321731)
XLA Ops:
  1.6 1.4 broadcast_select_fusion.1
  3.0 5.1 %fusion.12 = f32[4,640,192]{1,2,0:T(8,128)S(1)} fusion(bf16[4,640,1280]{2,1,0:T(8,128)(2,1)} %param.11, bf16[4,96,1280]{2,1,0:T(8,128)(2,1)S(1)} %get-tuple-element.10, bf16[4,96,1280]{2,1,0:T(8,128)(2,1)S(1)} %get-tuple-element.9), kind=kOutput, calls=%fused_computation.15 | convolution fusion | flops 1262223360 | bytes 10485760 | tf_op jit(solution)/shard_map/mji,mri->mjr/dot_general | solution.py:154
  11.9 7.3 %all-to-all-start = ((bf16[32,16,384]{2,1,0:T(8,128)(2,1)}), bf16[32,16,384]{2,1,0:T(8,128)(2,1)S(1)}, u32[]{:S(2)}, u32[]{:S(2)}) async-start(bf16[32,16,384]{2,1,0:T(8,128)(2,1)} %slice.45), calls=%async_computation | async-start | bytes 786432 | tf_op jit(solution)/shard_map/all_to_all | solution.py:173
  20.1 12.4 %all-to-all-done = bf16[32,16,384]{2,1,0:T(8,128)(2,1)S(1)} async-done(((bf16[32,16,384]{2,1,0:T(8,128)(2,1)}), bf16[32,16,384]{2,1,0:T(8,128)(2,1)S(1)}, u32[]{:S(2)}, u32[]{:S(2)}) %all-to-all-start) | async-done | bytes 393248 | tf_op jit(solution)/shard_map/all_to_all | solution.py:173
  32.5 2.6 %all-to-all-start.2 = ((bf16[32,24,384]{2,1,0:T(8,128)(2,1)}), bf16[32,24,384]{2,1,0:T(8,128)(2,1)S(1)}, u32[]{:S(2)}, u32[]{:S(2)}) async-start(bf16[32,24,384]{2,1,0:T(8,128)(2,1)} %slice.47), calls=%async_computation.2 | async-start | bytes 1179648 | tf_op jit(solution)/shard_map/all_to_all | solution.py:173
  35.1 1.0 constant_dynamic-slice_fusion
  36.5 1.1 broadcast_select_fusion.2
  41.3 1.4 reshape.200.weights_ref
  43.4 13.8 %shard_map.100 = bf16[16,64,192]{2,1,0:T(8,128)(2,1)} custom-call(s32[16]{0:T(128)} %bitcast.84, f32[16]{0:T(128)} %convert_divide_fusion.1.inv_ref, f32[32,128]{1,0:T(8,128)} %broadcast_in_dim.59.wave_ref, f32[16,2560]{1,0:T(8,128)} %slice.42.coef_ref, bf16[16,64,192]{2,1,0:T(8,128)(2,1)} %reshape.200.weights_ref), custom_call_target="tpu_custom_call" | custom-call | tf_op jit(solution)/shard_map/pallas_call | solution.py:98
  57.2 1.6 %copy.34 = bf16[16,1,2,32,192]{4,2,0,3,1:T(2,128)(2,1)S(1)} copy(bf16[16,1,2,32,192]{4,3,2,0,1:T(8,128)(2,1)} %bitcast.78) | data formatting | bytes 786432 | tf_op jit(solution)/shard_map/reshape | solution.py:180
  58.8 1.0 reshape.202
  59.8 6.0 %all-to-all-start.1 = ((bf16[32,16,384]{2,1,0:T(8,128)(2,1)}), bf16[32,16,384]{2,1,0:T(8,128)(2,1)S(1)}, u32[]{:S(2)}, u32[]{:S(2)}) async-start(bf16[32,16,384]{2,1,0:T(8,128)(2,1)} %reshape.202), calls=%async_computation.1 | async-start | bytes 786432 | tf_op jit(solution)/shard_map/all_to_all | solution.py:183
  67.9 1.3 reshape.203
  69.2 1.2 copy.24
  70.5 1.6 %reshape.204.weights_ref = bf16[24,64,192]{2,1,0:T(8,128)(2,1)} reshape(bf16[24,2,8,4,4,48]{5,4,3,2,1,0:T(4,128)(2,1)S(1)} %copy.24) | data formatting | bytes 1179648 | tf_op jit(solution)/shard_map/reshape | solution.py:178
  72.0 20.0 %shard_map.101 = bf16[24,64,192]{2,1,0:T(8,128)(2,1)} custom-call(s32[24]{0:T(128)} %slice.37.pts_ref, f32[24]{0:T(128)} %convert_divide_fusion.inv_ref, f32[32,128]{1,0:T(8,128)} %broadcast_in_dim.59.wave_ref, f32[24,2560]{1,0:T(8,128)} %slice.46.coef_ref, bf16[24,64,192]{2,1,0:T(8,128)(2,1)} %reshape.204.weights_ref), custom_call_target="tpu_custom_call" | custom-call | tf_op jit(solution)/shard_map/pallas_call | solution.py:98
  92.0 2.0 %copy.33 = bf16[24,1,2,32,192]{4,2,0,3,1:T(2,128)(2,1)S(1)} copy(bf16[24,1,2,32,192]{4,3,2,0,1:T(8,128)(2,1)} %bitcast.75) | data formatting | bytes 1179648 | tf_op jit(solution)/shard_map/reshape | solution.py:180
  94.0 1.2 reshape.206
  95.3 5.7 %all-to-all-start.3 = ((bf16[32,24,384]{2,1,0:T(8,128)(2,1)}), bf16[32,24,384]{2,1,0:T(8,128)(2,1)S(1)}, u32[]{:S(2)}, u32[]{:S(2)}) async-start(bf16[32,24,384]{2,1,0:T(8,128)(2,1)} %reshape.206), calls=%async_computation.3 | async-start | bytes 1179648 | tf_op jit(solution)/shard_map/all_to_all | solution.py:183
  104.4 13.3 %all-to-all-done.3 = bf16[32,24,384]{2,1,0:T(8,128)(2,1)S(1)} async-done(((bf16[32,24,384]{2,1,0:T(8,128)(2,1)}), bf16[32,24,384]{2,1,0:T(8,128)(2,1)S(1)}, u32[]{:S(2)}, u32[]{:S(2)}) %all-to-all-start.3) | async-done | bytes 589856 | tf_op jit(solution)/shard_map/all_to_all | solution.py:183
  118.3 2.4 %fusion.10 = bf16[384,1280]{1,0:T(8,128)(2,1)S(1)} fusion(bf16[640,384]{1,0:T(8,128)(2,1)S(1)} %bitcast.79, bf16[4,640,1280]{2,1,0:T(8,128)(2,1)} %param.11, s32[]{:T(128)S(6)} %select_n.78), kind=kOutput, calls=%fused_computation.13 | convolution fusion | flops 629145600 | bytes 3112964 | tf_op jit(solution)/shard_map/jr,ji->ri/dot_general | solution.py:197
  120.7 2.4 %fusion.3 = bf16[384,1280]{1,0:T(8,128)(2,1)S(1)} fusion(bf16[384,1280]{1,0:T(8,128)(2,1)S(1)} %fusion.10, bf16[640,384]{1,0:T(8,128)(2,1)S(1)} %bitcast.83, bf16[4,640,1280]{2,1,0:T(8,128)(2,1)} %param.11, s32[]{:T(128)S(6)} %select_n.78, pred[1280]{0:T(1024)(128)(4,1)S(1)} %copy-done.3, pred[1280]{0:T(1024)(128)(4,1)S(1)} %iota_compare_fusion.1), kind=kOutput, calls=%fused_computation.5 | convolution fusion | flops 630128640 | bytes 4098564 | tf_op jit(solution)/shard_map/jr,ji->ri/dot_general | solution.py:198
  125.0 19.7 %all_to_all.35 = bf16[6,64,1280]{2,0,1:T(8,128)(2,1)S(1)} all-to-all(bf16[6,64,1280]{2,0,1:T(8,128)(2,1)S(1)} %copy.27), channel_id=1, replica_groups=mesh['wave'=8,'lev'=4] {'lev'}, dimensions={1} | all-to-all | bytes 1966080 | tf_op jit(solution)/shard_map/all_to_all | solution.py:210
  144.7 1.1 copy.32
  (63 shorter events, 18.7 us)
Async XLA Ops:
  0.0 123.2 %copy-start = (bf16[64,64]{1,0:T(8,128)(2,1)S(1)}, bf16[64,64]{1,0:T(8,128)(2,1)}, u32[]{:S(2)}) copy-start(bf16[64,64]{1,0:T(8,128)(2,1)} %param.18) | copy-start | bytes 24580
  0.0 8.1 %copy-start.2 = (pred[1280]{0:T(1024)(128)(4,1)}, pred[1280]{0:T(1024)(128)(4,1)S(1)}, u32[]{:S(2)}) copy-start(pred[1280]{0:T(1024)(128)(4,1)S(1)} %get-tuple-element.14) | copy-start | bytes 3844
  11.0 9.1 %copy-start.9 = (s32[32]{0:T(128)S(1)}, s32[32]{0:T(128)}, u32[]{:S(2)}) copy-start(s32[32]{0:T(128)} %param.12) | copy-start | bytes 388
  11.9 20.6 %all-to-all-start = ((bf16[32,16,384]{2,1,0:T(8,128)(2,1)}), bf16[32,16,384]{2,1,0:T(8,128)(2,1)S(1)}, u32[]{:S(2)}, u32[]{:S(2)}) async-start(bf16[32,16,384]{2,1,0:T(8,128)(2,1)} %slice.45), calls=%async_computation | async-start | bytes 786432 | tf_op jit(solution)/shard_map/all_to_all | solution.py:173
  32.5 27.3 %all-to-all-start.2 = ((bf16[32,24,384]{2,1,0:T(8,128)(2,1)}), bf16[32,24,384]{2,1,0:T(8,128)(2,1)S(1)}, u32[]{:S(2)}, u32[]{:S(2)}) async-start(bf16[32,24,384]{2,1,0:T(8,128)(2,1)} %slice.47), calls=%async_computation.2 | async-start | bytes 1179648 | tf_op jit(solution)/shard_map/all_to_all | solution.py:173
  39.0 3.6 %copy-start.6 = (s32[40]{0:T(128)}, s32[40]{0:T(128)S(1)}, u32[]{:S(2)}) copy-start(s32[40]{0:T(128)S(1)} %dynamic_slice.27) | copy-start | bytes 484
  43.4 23.2 %copy-start.7 = (s32[40]{0:T(128)S(1)}, s32[40]{0:T(128)}, u32[]{:S(2)}) copy-start(s32[40]{0:T(128)} %copy-done.6) | copy-start | bytes 484
  59.8 35.5 %all-to-all-start.1 = ((bf16[32,16,384]{2,1,0:T(8,128)(2,1)}), bf16[32,16,384]{2,1,0:T(8,128)(2,1)S(1)}, u32[]{:S(2)}, u32[]{:S(2)}) async-start(bf16[32,16,384]{2,1,0:T(8,128)(2,1)} %reshape.202), calls=%async_computation.1 | async-start | bytes 786432 | tf_op jit(solution)/shard_map/all_to_all | solution.py:183
  92.0 8.9 %copy-start.8 = (s32[32]{0:T(128)S(1)}, s32[32]{0:T(128)}, u32[]{:S(2)}) copy-start(s32[32]{0:T(128)} %param.13) | copy-start | bytes 388
  92.0 9.6 %copy-start.10 = (s32[32]{0:T(128)S(1)}, s32[32]{0:T(128)}, u32[]{:S(2)}) copy-start(s32[32]{0:T(128)} %param.12) | copy-start | bytes 388
  92.0 10.2 %copy-start.4 = (f32[640]{0:T(1024)S(1)}, f32[640]{0:T(1024)}, u32[]{:S(2)}) copy-start(f32[640]{0:T(1024)} %param.16) | copy-start | bytes 7684
  92.0 12.2 %copy-start.5 = (f32[64]{0:T(128)S(1)}, f32[64]{0:T(128)}, u32[]{:S(2)}) copy-start(f32[64]{0:T(128)} %param.19) | copy-start | bytes 772
  95.3 22.5 %all-to-all-start.3 = ((bf16[32,24,384]{2,1,0:T(8,128)(2,1)}), bf16[32,24,384]{2,1,0:T(8,128)(2,1)S(1)}, u32[]{:S(2)}, u32[]{:S(2)}) async-start(bf16[32,24,384]{2,1,0:T(8,128)(2,1)} %reshape.206), calls=%async_computation.3 | async-start | bytes 1179648 | tf_op jit(solution)/shard_map/all_to_all | solution.py:183
  118.2 2.4 %copy-start.3 = (pred[1280]{0:T(1024)(128)(4,1)S(1)}, pred[1280]{0:T(1024)(128)(4,1)}, u32[]{:S(2)}) copy-start(pred[1280]{0:T(1024)(128)(4,1)} %copy-done.2) | copy-start | bytes 3844
  123.1 0.7 copy-start.1

commit v3 on v2

--- a/solution.py
+++ b/solution.py
@@ -8,7 +8,7 @@
 from jax.sharding import PartitionSpec as P
 
 LANES = 128
-UNROLL = 2
+UNROLL = 8
 CHUNK = 512
 
 
@@ -26,7 +26,9 @@
     return cosine * sign, sine * angle * sign
 
 
-def grid_kernel(pts_ref, inv_ref, wave_ref, coef_ref, weights_ref, out_ref, table, tend, *, items):
+def grid_kernel(
+    pts_ref, inv_ref, flip_ref, wave_ref, coef_ref, weights_ref, out_ref, table, tend, *, items, first
+):
     waves = wave_ref.shape[0]
     points = coef_ref.shape[1]
     rows = weights_ref.shape[2]
@@ -35,9 +37,9 @@
     lane_f = lane.astype(jnp.float32)
 
     def one(pos, slot):
-        pts = pts_ref[pos]
+        pts = pts_ref[first + pos]
         pts_f = pts.astype(jnp.float32)
-        inv = inv_ref[pos]
+        inv = inv_ref[first + pos]
         prod = wave * lane_f
         left = prod - jnp.floor(prod * inv) * pts_f
         cosine, sine = unit_circle(left * inv)
@@ -58,18 +60,19 @@
                 sine * step_c - cosine * step_s,
             )
         weights = weights_ref[pos]
+        row = jnp.where(flip_ref[0] == 1, coef_ref.shape[0] - 1 - first - pos, first + pos)
         for start in range(0, points, CHUNK):
             cols = slice(start, start + CHUNK)
             grid = lax.dot_general(
                 weights, table[slot, :, cols], (((0,), (0,)), ((), ())),
                 preferred_element_type=jnp.float32,
             )
-            coef = coef_ref[pl.ds(pos, 1), cols]
-            for first in range(0, rows, 3 * items):
-                parts = [grid[first + f * items:first + (f + 1) * items] for f in range(3)]
+            coef = coef_ref[pl.ds(row, 1), cols]
+            for base in range(0, rows, 3 * items):
+                parts = [grid[base + f * items:base + (f + 1) * items] for f in range(3)]
                 for f in range(3):
                     value = parts[f] * (coef + parts[(f + 1) % 3])
-                    low = first + f * items
+                    low = base + f * items
                     tend[slot, low:low + items, cols] = value.astype(jnp.bfloat16)
         back = lax.dot_general(
             table[slot], tend[slot], (((1,), (1,)), ((), ())),
@@ -77,7 +80,7 @@
         )
         out_ref[pos] = (back * inv).astype(jnp.bfloat16)
 
-    count = coef_ref.shape[0]
+    count = weights_ref.shape[0]
     together = UNROLL if count % UNROLL == 0 else 1
 
     def step(index, carry):
@@ -88,23 +91,39 @@
     lax.fori_loop(0, count // together, step, 0)
 
 
-def grid_trip(weights, wave_ids, counts, coefs, items):
+def grid_trip(weights, wave_f, counts, inverse, flip, coefs, items, first):
     count, modes, rows = weights.shape
-    waves = wave_ids.shape[0]
     points = coefs.shape[1]
-    wave_f = jnp.broadcast_to(wave_ids.astype(jnp.float32)[:, None], (waves, LANES))
     smem = pl.BlockSpec(memory_space=pltpu.SMEM)
     vmem = pl.BlockSpec(memory_space=pltpu.VMEM)
     return pl.pallas_call(
-        functools.partial(grid_kernel, items=items),
-        in_specs=[smem, smem, vmem, vmem, vmem],
+        functools.partial(grid_kernel, items=items, first=first),
+        in_specs=[smem, smem, smem, vmem, vmem, vmem],
         out_specs=vmem,
         out_shape=jax.ShapeDtypeStruct((count, modes, rows), jnp.bfloat16),
         scratch_shapes=[
             pltpu.VMEM((UNROLL, modes, points), jnp.bfloat16),
             pltpu.VMEM((UNROLL, rows, points), jnp.bfloat16),
         ],
-    )(counts, 1.0 / counts.astype(jnp.float32), wave_f, coefs, weights)
+    )(counts, inverse, flip, wave_f, coefs, weights)
+
+
+def trade_levels(update, lev_size, lev_rank):
+    share, levels, spec_len = update.shape
+    lev_local = levels // lev_size
+
+    def piece(rank):
+        return lax.dynamic_slice_in_dim(update, rank * lev_local, lev_local, 1)
+
+    joined = jnp.zeros((lev_size * share, lev_local, spec_len), update.dtype)
+    joined = lax.dynamic_update_slice_in_dim(joined, piece(lev_rank), lev_rank * share, 0)
+    arrived = []
+    for mask in [*range(2, lev_size), 1]:
+        pairs = [(rank, rank ^ mask) for rank in range(lev_size)]
+        arrived.append((mask, lax.ppermute(piece(lev_rank ^ mask), "lev", pairs)))
+    for mask, got in arrived:
+        joined = lax.dynamic_update_slice_in_dim(joined, got, (lev_rank ^ mask) * share, 0)
+    return joined
 
 
 def on_device(
@@ -142,7 +161,9 @@
     counts = lax.dynamic_slice_in_dim(cycle_points, north_rank * band + lev_rank * sub, sub)
     coef_row = jnp.where(flip, band - (lev_rank + 1) * sub, lev_rank * sub)
     coefs = lax.dynamic_slice_in_dim(grid_coef, coef_row, sub, 0)
-    coefs = jnp.where(flip, coefs[::-1], coefs)
+    inverse = 1.0 / counts.astype(jnp.float32)
+    flipped = flip.astype(jnp.int32)[None]
+    wave_f = jnp.broadcast_to(wave_ids.astype(jnp.float32)[:, None], (wave_total, LANES))
 
     factor = jnp.where(own_waves == 0, 1.0, 2.0).astype(jnp.bfloat16)
     live = (position[None, :] < own_lengths[:, None])[:, None, :]
@@ -176,7 +197,7 @@
         weights = got.reshape(wave_size, lev_size, size, wave_local, 2, fields * lev_local)
         weights = weights.transpose(2, 4, 0, 3, 1, 5)
         weights = weights.reshape(size, 2 * wave_total, fields * levels)
-        analysed = grid_trip(weights, wave_ids, counts[low:high], coefs[low:high], lev_local)
+        analysed = grid_trip(weights, wave_f, counts, inverse, flipped, coefs, lev_local, low)
         sent = analysed.reshape(size, 2 // parts_of_r, parts_of_r, wave_total, fields * levels)
         sent = sent.transpose(3, 1, 0, 2, 4).reshape(everyone, size, share * levels)
         pieces.append(
@@ -207,7 +228,7 @@
     update = jnp.einsum(
         "lq,cqi->cli", modes_out, scaled, preferred_element_type=jnp.float32
     ).astype(jnp.bfloat16)
-    update = lax.all_to_all(update, "lev", split_axis=1, concat_axis=0, tiled=True)
+    update = trade_levels(update, lev_size, lev_rank)
     return update.reshape(wave_local, channels, lev_local, spec_len)
 
 

time: 147 us -> 151 us (1.027)
  blocking collectives: 19.7 us -> 0 us
  local copies, waits for them, and re-layouts: 27 us -> 43.4 us
  waiting for transfers between devices: 25.7 us -> 33.4 us
  Pallas kernels: 33.8 us -> 28.5 us
  starting transfers between devices: 21.6 us -> 24.2 us
    all_to_all x1 -> x0, blocking collectives: 19.7 us -> none  [on_device(): lax.all_to_all(update, 'lev', split_axis=1, concat_axis=0, tiled=True)]
    ppermute x0 -> x3, waiting for transfers between devices: none -> 8.92 us  [trade_levels(): arrived.append((mask, lax.ppermute(piece(lev_rank ^ mask), 'lev', pairs)))]
    reshape x2, local copies, waits for them, and re-layouts: 2.21 us -> 10.9 us  [on_device(): got.reshape(wave_size, lev_size, size, wave_local, 2, fields * lev_local)]
    pallas_call x2, Pallas kernels: 33.8 us -> 28.5 us  [grid_trip(): pl.pallas_call(functools.partial(grid_kernel, items=items, first=first),...]
    unnamed x23 -> x25, local copies, waits for them, and re-layouts: 0.7 us -> 4.46 us
    reshape x2, local copies, waits for them, and re-layouts: 3 us -> 6.1 us  [on_device(): weights = weights.reshape(size, 2 * wave_total, fields * levels)]
    ppermute x0 -> x3, starting transfers between devices: none -> 2.21 us  [trade_levels(): arrived.append((mask, lax.ppermute(piece(lev_rank ^ mask), 'lev', pairs)))]
    transpose x2, local copies, waits for them, and re-layouts: 2.03 us -> 4.21 us  [on_device(): weights = weights.transpose(2, 4, 0, 3, 1, 5)]
  transfers between devices with their start and end apart: 4 -> 7, of which waited for: 2 -> 4; matrix products, arithmetic and copies ran while one was open for 17% -> 24% of each run, Pallas kernels for 23% -> 19%
where the time goes in v3:
time: 151 us; the launch traced here: 150 us
  local copies, waits for them, and re-layouts  43.4 us (29%)
  waiting for transfers between devices  33.4 us (22%)
  Pallas kernels  28.5 us (19%)
  starting transfers between devices  24.2 us (16%)
  matrix products  11.8 us (8%)
  other arithmetic  8.16 us (5%)
    pallas_call x2, Pallas kernels, grid_trip(): pl.pallas_call(functools.partial(grid_kernel, items=items, first=first),...  28.5 us
    all_to_all x2, waiting for transfers between devices, on_device(): lax.all_to_all(blocks[:, low:high], ('wave', 'lev'), split_axis=0, concat...  12.4 us
    all_to_all x2, waiting for transfers between devices, on_device(): lax.all_to_all(sent, ('wave', 'lev'), split_axis=0, concat_axis=0, tiled=...  12.1 us
    all_to_all x2, starting transfers between devices, on_device(): lax.all_to_all(sent, ('wave', 'lev'), split_axis=0, concat_axis=0, tiled=...  11.8 us
    reshape x2, local copies, waits for them, and re-layouts, on_device(): got.reshape(wave_size, lev_size, size, wave_local, 2, fields * lev_local)  10.9 us
    all_to_all x2, starting transfers between devices, on_device(): lax.all_to_all(blocks[:, low:high], ('wave', 'lev'), split_axis=0, concat...  10.1 us
    ppermute x3, waiting for transfers between devices, trade_levels(): arrived.append((mask, lax.ppermute(piece(lev_rank ^ mask), 'lev', pairs)))  8.92 us
    reshape x2, local copies, waits for them, and re-layouts, on_device(): weights = weights.reshape(size, 2 * wave_total, fields * levels)  6.1 us
  transfers between devices with their start and end apart: 7, of which 4 were waited for; matrix products, arithmetic and copies ran while one was open for 24% of the time, Pallas kernels for 19%

profile of v3, /device:TPU:0, one launch (start us, length us, event | category | flops | bytes accessed | tf_op | source)
XLA Modules:
  0.0 149.8 jit_solution(9120482222233880731)
XLA Ops:
  1.7 1.4 broadcast_select_fusion.1
  3.1 5.1 %fusion.11 = f32[4,640,192]{1,2,0:T(8,128)S(1)} fusion(bf16[4,640,1280]{2,1,0:T(8,128)(2,1)} %param.11, bf16[4,96,1280]{2,1,0:T(8,128)(2,1)S(1)} %get-tuple-element.12, bf16[4,96,1280]{2,1,0:T(8,128)(2,1)S(1)} %get-tuple-element.11), kind=kOutput, calls=%fused_computation.14 | convolution fusion | flops 1262223360 | bytes 10485760 | tf_op jit(solution)/shard_map/mji,mri->mjr/dot_general | solution.py:175
  14.6 7.3 %all-to-all-start = ((bf16[32,16,384]{2,1,0:T(8,128)(2,1)}), bf16[32,16,384]{2,1,0:T(8,128)(2,1)S(1)}, u32[]{:S(2)}, u32[]{:S(2)}) async-start(bf16[32,16,384]{2,1,0:T(8,128)(2,1)} %slice.28), calls=%async_computation | async-start | bytes 786432 | tf_op jit(solution)/shard_map/all_to_all | solution.py:194
  22.8 12.4 %all-to-all-done = bf16[32,16,384]{2,1,0:T(8,128)(2,1)S(1)} async-done(((bf16[32,16,384]{2,1,0:T(8,128)(2,1)}), bf16[32,16,384]{2,1,0:T(8,128)(2,1)S(1)}, u32[]{:S(2)}, u32[]{:S(2)}) %all-to-all-start) | async-done | bytes 393248 | tf_op jit(solution)/shard_map/all_to_all | solution.py:194
  35.9 2.8 %all-to-all-start.2 = ((bf16[32,24,384]{2,1,0:T(8,128)(2,1)}), bf16[32,24,384]{2,1,0:T(8,128)(2,1)S(1)}, u32[]{:S(2)}, u32[]{:S(2)}) async-start(bf16[32,24,384]{2,1,0:T(8,128)(2,1)} %slice.29), calls=%async_computation.2 | async-start | bytes 1179648 | tf_op jit(solution)/shard_map/all_to_all | solution.py:194
  38.8 1.3 convert_divide_fusion
  40.9 4.6 %reshape.200 = bf16[8,4,16,4,2,48]{5,4,3,2,1,0:T(2,128)(2,1)S(1)} reshape(bf16[32,16,384]{2,1,0:T(8,128)(2,1)} %copy-done.4) | data formatting | bytes 786432 | tf_op jit(solution)/shard_map/reshape | solution.py:197
  45.5 1.8 %copy.13 = bf16[16,2,8,4,4,48]{5,4,3,2,1,0:T(4,128)(2,1)} copy(bf16[16,2,8,4,4,48]{5,1,3,0,4,2:T(2,128)(2,1)S(1)} %bitcast.73) | data formatting | bytes 786432 | tf_op jit(solution)/shard_map/transpose | solution.py:198
  47.3 2.6 %reshape.201.weights_ref = bf16[16,64,192]{2,1,0:T(8,128)(2,1)} reshape(bf16[16,2,8,4,4,48]{5,4,3,2,1,0:T(4,128)(2,1)} %copy.13) | data formatting | bytes 786432 | tf_op jit(solution)/shard_map/reshape | solution.py:199
  50.5 11.7 %shard_map.100 = bf16[16,64,192]{2,1,0:T(8,128)(2,1)} custom-call(s32[40]{0:T(128)} %get-tuple-element.6.pts_ref, f32[40]{0:T(128)} %get-tuple-element.5.inv_ref, s32[1]{0:T(128)} %bitcast.1.flip_ref, f32[32,128]{1,0:T(8,128)} %broadcast_in_dim.66.wave_ref, f32[40,2560]{1,0:T(8,128)} %constant_dynamic-slice_fusion.coef_ref, ...), custom_call_target="tpu_custom_call" | custom-call | tf_op jit(solution)/shard_map/pallas_call | solution.py:99
  62.2 1.6 %copy.21 = bf16[16,1,2,32,192]{4,2,0,3,1:T(2,128)(2,1)S(1)} copy(bf16[16,1,2,32,192]{4,3,2,0,1:T(8,128)(2,1)} %bitcast.79) | data formatting | bytes 786432 | tf_op jit(solution)/shard_map/reshape | solution.py:201
  65.7 6.0 %all-to-all-start.1 = ((bf16[32,16,384]{2,1,0:T(8,128)(2,1)}), bf16[32,16,384]{2,1,0:T(8,128)(2,1)}, u32[]{:S(2)}, u32[]{:S(2)}) async-start(bf16[32,16,384]{2,1,0:T(8,128)(2,1)} %reshape.203), calls=%async_computation.1 | async-start | bytes 786432 | tf_op jit(solution)/shard_map/all_to_all | solution.py:204
  71.7 6.4 %reshape.204 = bf16[8,4,24,4,2,48]{5,4,3,2,1,0:T(2,128)(2,1)S(1)} reshape(bf16[32,24,384]{2,1,0:T(8,128)(2,1)} %copy-done.1) | data formatting | bytes 1179648 | tf_op jit(solution)/shard_map/reshape | solution.py:197
  78.1 2.4 %copy.15 = bf16[24,2,8,4,4,48]{5,4,3,2,1,0:T(4,128)(2,1)} copy(bf16[24,2,8,4,4,48]{5,1,3,0,4,2:T(2,128)(2,1)S(1)} %bitcast.72) | data formatting | bytes 1179648 | tf_op jit(solution)/shard_map/transpose | solution.py:198
  80.5 3.5 %reshape.205.weights_ref = bf16[24,64,192]{2,1,0:T(8,128)(2,1)} reshape(bf16[24,2,8,4,4,48]{5,4,3,2,1,0:T(4,128)(2,1)} %copy.15) | data formatting | bytes 1179648 | tf_op jit(solution)/shard_map/reshape | solution.py:199
  84.0 16.8 %shard_map.101 = bf16[24,64,192]{2,1,0:T(8,128)(2,1)} custom-call(s32[40]{0:T(128)} %get-tuple-element.6.pts_ref, f32[40]{0:T(128)} %get-tuple-element.5.inv_ref, s32[1]{0:T(128)} %bitcast.1.flip_ref, f32[32,128]{1,0:T(8,128)} %broadcast_in_dim.66.wave_ref, f32[40,2560]{1,0:T(8,128)} %constant_dynamic-slice_fusion.coef_ref, ...), custom_call_target="tpu_custom_call" | custom-call | tf_op jit(solution)/shard_map/pallas_call | solution.py:99
  100.8 2.0 %copy.20 = bf16[24,1,2,32,192]{4,2,0,3,1:T(2,128)(2,1)S(1)} copy(bf16[24,1,2,32,192]{4,3,2,0,1:T(8,128)(2,1)} %bitcast.77) | data formatting | bytes 1179648 | tf_op jit(solution)/shard_map/reshape | solution.py:201
  104.0 5.8 %all-to-all-start.3 = ((bf16[32,24,384]{2,1,0:T(8,128)(2,1)}), bf16[32,24,384]{2,1,0:T(8,128)(2,1)S(1)}, u32[]{:S(2)}, u32[]{:S(2)}) async-start(bf16[32,24,384]{2,1,0:T(8,128)(2,1)} %reshape.207), calls=%async_computation.3 | async-start | bytes 1179648 | tf_op jit(solution)/shard_map/all_to_all | solution.py:204
  114.3 12.1 %all-to-all-done.3 = bf16[32,24,384]{2,1,0:T(8,128)(2,1)S(1)} async-done(((bf16[32,24,384]{2,1,0:T(8,128)(2,1)}), bf16[32,24,384]{2,1,0:T(8,128)(2,1)S(1)}, u32[]{:S(2)}, u32[]{:S(2)}) %all-to-all-start.3) | async-done | bytes 589856 | tf_op jit(solution)/shard_map/all_to_all | solution.py:204
  128.8 2.4 %fusion.9 = bf16[384,1280]{1,0:T(8,128)(2,1)S(1)} fusion(bf16[640,384]{1,0:T(8,128)(2,1)S(1)} %bitcast.81, bf16[4,640,1280]{2,1,0:T(8,128)(2,1)} %param.11, s32[]{:T(128)S(6)} %select_n.94), kind=kOutput, calls=%fused_computation.12 | convolution fusion | flops 629145600 | bytes 3112964 | tf_op jit(solution)/shard_map/jr,ji->ri/dot_general | solution.py:218
  131.2 2.4 %fusion.3 = bf16[384,1280]{1,0:T(8,128)(2,1)S(1)} fusion(bf16[384,1280]{1,0:T(8,128)(2,1)S(1)} %fusion.9, bf16[640,384]{1,0:T(8,128)(2,1)S(1)} %bitcast.85, bf16[4,640,1280]{2,1,0:T(8,128)(2,1)} %param.11, s32[]{:T(128)S(6)} %select_n.94, pred[1280]{0:T(1024)(128)(4,1)S(1)} %get-tuple-element.19, pred[1280]{0:T(1024)(128)(4,1)S(1)} %iota_compare_fusion.1), kind=kOutput, calls=%fused_computation.5 | convolution fusion | flops 630128640 | bytes 4098564 | tf_op jit(solution)/shard_map/jr,ji->ri/dot_general | solution.py:219
  134.7 1.8 %convolution_convert_fusion = bf16[6,1280,64]{1,2,0:T(8,128)(2,1)S(1)} fusion(bf16[6,64,1280]{2,1,0:T(8,128)(2,1)} %bitcast.76, f32[64,1280]{1,0:T(8,128)S(1)} %add_divide_fusion, bf16[64,64]{1,0:T(8,128)(2,1)S(1)} %copy-done.6, bf16[64,64]{1,0:T(8,128)(2,1)S(1)} %copy-done.7), kind=kOutput, calls=%fused_computation.6 | convolution fusion | flops 127303680 | bytes 2310144 | tf_op jit(solution)/shard_map/lq,cqi->cli/dot_general | solution.py:228
  138.9 6.7 %collective-permute-done = bf16[6,16,1280]{2,1,0:T(8,128)(2,1)} collective-permute-done((bf16[6,16,1280]{2,1,0:T(8,128)(2,1)S(1)}, bf16[6,16,1280]{2,1,0:T(8,128)(2,1)}, u32[]{:S(2)}, u32[]{:S(2)}) %collective-permute-start) | collective-permute-done | bytes 245792 | tf_op jit(solution)/shard_map/ppermute | solution.py:123
  146.6 2.2 %collective-permute-done.1 = bf16[6,16,1280]{2,1,0:T(8,128)(2,1)S(1)} collective-permute-done((bf16[6,16,1280]{2,1,0:T(8,128)(2,1)S(1)}, bf16[6,16,1280]{2,1,0:T(8,128)(2,1)S(1)}, u32[]{:S(2)}, u32[]{:S(2)}) %collective-permute-start.1) | collective-permute-done | bytes 245792 | tf_op jit(solution)/shard_map/ppermute | solution.py:123
  (67 shorter events, 26.3 us)
Async XLA Ops:
  0.0 40.1 %copy-start = (f32[160,2560]{1,0:T(8,128)S(1)}, f32[160,2560]{1,0:T(8,128)}, u32[]{:S(2)}) copy-start(f32[160,2560]{1,0:T(8,128)} %param.15) | copy-start | bytes 4915204
  10.5 2.1 %copy-start.2 = (bf16[4,4,40,384]{3,2,1,0:T(8,128)(2,1)S(1)}, bf16[4,4,40,384]{3,2,1,0:T(8,128)(2,1)}, u32[]{:S(2)}) copy-start(bf16[4,4,40,384]{3,2,1,0:T(8,128)(2,1)} %rev.6) | copy-start | bytes 1474564
  13.8 25.0 %copy-start.11 = (s32[32]{0:T(128)S(1)}, s32[32]{0:T(128)}, u32[]{:S(2)}) copy-start(s32[32]{0:T(128)} %param.12) | copy-start | bytes 388
  14.6 20.6 %all-to-all-start = ((bf16[32,16,384]{2,1,0:T(8,128)(2,1)}), bf16[32,16,384]{2,1,0:T(8,128)(2,1)S(1)}, u32[]{:S(2)}, u32[]{:S(2)}) async-start(bf16[32,16,384]{2,1,0:T(8,128)(2,1)} %slice.28), calls=%async_computation | async-start | bytes 786432 | tf_op jit(solution)/shard_map/all_to_all | solution.py:194
  35.1 0.8 copy-start.4
  35.9 29.0 %all-to-all-start.2 = ((bf16[32,24,384]{2,1,0:T(8,128)(2,1)}), bf16[32,24,384]{2,1,0:T(8,128)(2,1)S(1)}, u32[]{:S(2)}, u32[]{:S(2)}) async-start(bf16[32,24,384]{2,1,0:T(8,128)(2,1)} %slice.29), calls=%async_computation.2 | async-start | bytes 1179648 | tf_op jit(solution)/shard_map/all_to_all | solution.py:194
  64.9 0.8 copy-start.1
  65.7 38.3 %all-to-all-start.1 = ((bf16[32,16,384]{2,1,0:T(8,128)(2,1)}), bf16[32,16,384]{2,1,0:T(8,128)(2,1)}, u32[]{:S(2)}, u32[]{:S(2)}) async-start(bf16[32,16,384]{2,1,0:T(8,128)(2,1)} %reshape.203), calls=%async_computation.1 | async-start | bytes 786432 | tf_op jit(solution)/shard_map/all_to_all | solution.py:204
  100.8 9.1 %copy-start.10 = (s32[32]{0:T(128)S(1)}, s32[32]{0:T(128)}, u32[]{:S(2)}) copy-start(s32[32]{0:T(128)} %param.13) | copy-start | bytes 388
  100.8 10.3 %copy-start.8 = (f32[640]{0:T(1024)S(1)}, f32[640]{0:T(1024)}, u32[]{:S(2)}) copy-start(f32[640]{0:T(1024)} %param.16) | copy-start | bytes 7684
  100.8 12.3 %copy-start.9 = (f32[64]{0:T(128)S(1)}, f32[64]{0:T(128)}, u32[]{:S(2)}) copy-start(f32[64]{0:T(128)} %param.19) | copy-start | bytes 772
  104.0 22.4 %all-to-all-start.3 = ((bf16[32,24,384]{2,1,0:T(8,128)(2,1)}), bf16[32,24,384]{2,1,0:T(8,128)(2,1)S(1)}, u32[]{:S(2)}, u32[]{:S(2)}) async-start(bf16[32,24,384]{2,1,0:T(8,128)(2,1)} %reshape.207), calls=%async_computation.3 | async-start | bytes 1179648 | tf_op jit(solution)/shard_map/all_to_all | solution.py:204
  126.5 0.9 copy-start.3
  133.6 1.1 copy-start.6
  133.6 1.0 copy-start.7
  136.6 9.0 %collective-permute-start = (bf16[6,16,1280]{2,1,0:T(8,128)(2,1)S(1)}, bf16[6,16,1280]{2,1,0:T(8,128)(2,1)}, u32[]{:S(2)}, u32[]{:S(2)}) collective-permute-start(bf16[6,16,1280]{2,1,0:T(8,128)(2,1)S(1)} %get-tuple-element.15), channel_id=1, source_target_pairs={{0,2},{1,3},{2,0},{3,1},{4,6},{5,7},{6,4},{7,5},{8,10},{9,11},{10,... | collective-permute-start | bytes 737288 | tf_op jit(solution)/shard_map/ppermute | solution.py:123
  137.7 11.1 %collective-permute-start.1 = (bf16[6,16,1280]{2,1,0:T(8,128)(2,1)S(1)}, bf16[6,16,1280]{2,1,0:T(8,128)(2,1)S(1)}, u32[]{:S(2)}, u32[]{:S(2)}) collective-permute-start(bf16[6,16,1280]{2,1,0:T(8,128)(2,1)S(1)} %get-tuple-element.14), channel_id=1, source_target_pairs={{0,3},{1,2},{2,1},{3,0},{4,7},{5,6},{6,5},{7,4},{8,11},{9,10},{10,... | collective-permute-start | bytes 737288 | tf_op jit(solution)/shard_map/ppermute | solution.py:123
  138.0 10.8 %collective-permute-start.2 = (bf16[6,16,1280]{2,1,0:T(8,128)(2,1)S(1)}, bf16[6,16,1280]{2,1,0:T(8,128)(2,1)S(1)}, u32[]{:S(2)}, u32[]{:S(2)}) collective-permute-start(bf16[6,16,1280]{2,1,0:T(8,128)(2,1)S(1)} %get-tuple-element.13), channel_id=1, source_target_pairs={{0,1},{1,0},{2,3},{3,2},{4,5},{5,4},{6,7},{7,6},{8,9},{9,8},{10,11... | collective-permute-start | bytes 737288 | tf_op jit(solution)/shard_map/ppermute | solution.py:123
  148.9 0.9 copy-start.5
